TPU v7x, 256 devices: a whole 4x4x8 slice. The times are simulated.
256 devices in a mesh: section: 16 (over y, z_hi, core), rep: 4 (over z_lo), sub: 4 (over x).
Axes of the slice: x: 4, y: 4, z: 8 (z_hi: 2, z_lo: 4; z = z_hi * 4 + z_lo), core: 2. Of those that a mesh axis runs over, the one named last changes fastest.
Arguments:
- token_ids: int32 [8, 512], P(None, ('rep', 'sub')), may hold values from 0 to 255
- target_ids: int32 [8, 512], P(None, ('rep', 'sub')), may hold values from 0 to 255
- embedding: bfloat16 [256, 2048], P(('rep', 'sub')), may hold values from -3 to 3
- section_weight: bfloat16 [16, 2048, 2048], P('section', ('rep', 'sub')), may hold values from -0.125 to 0.125
- section_gain: float32 [16, 2048], P('section'), may hold values from 0.1 to 1.9
- final_gain: float32 [2048], replicated, may hold values from 0.5 to 1.5
Outputs:
- weight_grad: float32 [16, 2048, 2048], P('section', ('rep', 'sub'))
- gain_grad: float32 [16, 2048], P('section')
- embed_grad: float32 [256, 2048], P(('section', 'rep', 'sub'))
- final_grad: float32 [2048], replicated
All inputs are finite; a program needn't handle non-finite values.
Results may differ from a plain program's by a relative error of at most 0.024.
Values may be sent and summed in bfloat16 or wider, within the bound.
No kernel may reach another device: no remote copies, remote signals or barrier semaphores. Data moves between devices by JAX's collectives and lax.ppermute only.
A program may use at most 64 MiB of HBM per device.

v0:
```python
import jax
import jax.numpy as jnp
from jax import lax
from jax.sharding import PartitionSpec as P

epsilon = 1e-06
gelu_coef = 0.7978845608028654
cube_coef = 0.044715


def passed_along(value, axis, steps):
    count = lax.axis_size(axis)
    initial, last = (max(0, -steps), min(count, count - steps))
    return lax.ppermute(value, axis, [(source, source + steps) for source in range(initial, last)])


def gelu(pre_act):
    return (
        0.5
        * pre_act
        * (1.0 + jnp.tanh(gelu_coef * (pre_act + cube_coef * pre_act * pre_act * pre_act)))
    )


def gelu_slope(pre_act):
    inside = gelu_coef * (pre_act + cube_coef * pre_act * pre_act * pre_act)
    tangent = jnp.tanh(inside)
    return 0.5 * (1.0 + tangent) + 0.5 * pre_act * (1.0 - tangent * tangent) * gelu_coef * (
        1.0 + 3.0 * cube_coef * pre_act * pre_act
    )


def normalize(residual, gain_row):
    values = residual.astype(jnp.float32)
    scale_inv = lax.rsqrt(jnp.mean(values * values, axis=-1, keepdims=True) + epsilon)
    normed = values * scale_inv
    return (normed, scale_inv, (normed * gain_row).astype(jnp.bfloat16))


def norm_back(grad_norm, normed, scale_inv, gain_row):
    grad_unit = grad_norm * gain_row
    grad_in = scale_inv * (
        grad_unit - normed * jnp.mean(grad_unit * normed, axis=-1, keepdims=True)
    )
    return (grad_in, jnp.sum(grad_norm * normed, axis=0))


def pick_slot(buffer, slot_index):
    return lax.dynamic_index_in_dim(buffer, slot_index, 0, keepdims=False)


def place_slot(buffer, update, slot_index):
    return lax.dynamic_update_index_in_dim(buffer, update, slot_index, 0)


def body(token_ids, target_ids, embedding, section_weight, section_gain, final_gain):
    sections = lax.axis_size("section")
    position = lax.axis_index("section")
    micro_count = token_ids.shape[0]
    row_count = token_ids.shape[1]
    features = embedding.shape[1]
    group_size = lax.axis_size(("rep", "sub"))
    vocab_rows = embedding.shape[0] * group_size
    tick_count = micro_count + sections - 1
    contract_last = (((1,), (1,)), ((), ()))
    contract_first = (((0,), (0,)), ((), ()))
    vocab_table = lax.all_gather(embedding, ("rep", "sub"), axis=0, tiled=True)
    weight = lax.all_gather(section_weight, ("rep", "sub"), axis=1, tiled=True)[0]
    gain_row = section_gain[0]
    is_first = position == 0
    is_last = position == sections - 1
    vocab_iota = jnp.arange(vocab_rows, dtype=jnp.int32)
    onehot_in = (token_ids.reshape(-1)[:, None] == vocab_iota[None, :]).astype(jnp.bfloat16)
    embedded = jnp.dot(onehot_in, vocab_table, preferred_element_type=jnp.float32).astype(
        jnp.bfloat16
    )
    embedded = embedded.reshape(micro_count, row_count, features)
    empty_rows = jnp.zeros((row_count, features), jnp.bfloat16)
    zeros_stash = jnp.zeros((micro_count, row_count, features), jnp.bfloat16)
    zeros_pre = jnp.zeros((micro_count, row_count, features), jnp.float32)

    def forward_tick(carried, tick_index):
        arrived = carried[0]
        buffers = carried[1:]
        offset = tick_index - position
        active = (offset >= 0) & (offset < micro_count)
        slot_index = jnp.clip(offset, 0, micro_count - 1)
        residual = jnp.where(is_first, pick_slot(embedded, slot_index), arrived)

        def forward_compute(kept_activations):
            input_list, rounded_list, preactivation_list, output_list = kept_activations
            normed, scale_inv, rounded = normalize(residual, gain_row)
            pre_act = jnp.dot(rounded, weight, preferred_element_type=jnp.float32)
            returned_value = (residual.astype(jnp.float32) + gelu(pre_act)).astype(jnp.bfloat16)
            kept_activations = (
                place_slot(input_list, residual, slot_index),
                place_slot(rounded_list, rounded, slot_index),
                place_slot(preactivation_list, pre_act, slot_index),
                place_slot(output_list, returned_value, slot_index),
            )
            return (kept_activations, returned_value)

        def forward_bypass(kept_activations):
            return (kept_activations, empty_rows)

        buffers, returned_value = lax.cond(active, forward_compute, forward_bypass, buffers)
        arrived = passed_along(returned_value, "section", 1)
        return ((arrived,) + buffers, None)

    start_state = (empty_rows, zeros_stash, zeros_stash, zeros_pre, zeros_stash)
    final_state, unused_out = lax.scan(
        forward_tick, start_state, jnp.arange(tick_count, dtype=jnp.int32)
    )
    input_list, rounded_list, preactivation_list, output_list = final_state[1:]
    logit_scale = float(features) ** (-0.5)

    def head(finals):
        normed, scale_inv, final_rows = normalize(finals, final_gain)
        logits = (
            lax.dot_general(
                final_rows, vocab_table, contract_last, preferred_element_type=jnp.float32
            )
            * logit_scale
        )
        exp_logit = jnp.exp(logits)
        probability = exp_logit / jnp.sum(exp_logit, axis=-1, keepdims=True)
        onehot_out = (target_ids.reshape(-1)[:, None] == vocab_iota[None, :]).astype(jnp.float32)
        grad_logit = ((probability - onehot_out) * logit_scale).astype(jnp.bfloat16)
        embed_head = lax.dot_general(
            grad_logit, final_rows, contract_first, preferred_element_type=jnp.float32
        )
        grad_final = jnp.dot(grad_logit, vocab_table, preferred_element_type=jnp.float32)
        grad_in, final_part = norm_back(grad_final, normed, scale_inv, final_gain)
        grad_top = grad_in.astype(jnp.bfloat16).reshape(micro_count, row_count, features)
        return (embed_head, grad_top, final_part)

    def no_head(finals):
        return (
            jnp.zeros((vocab_rows, features), jnp.float32),
            zeros_stash,
            jnp.zeros((features,), jnp.float32),
        )

    embed_head, grad_top, final_part = lax.cond(
        is_last, head, no_head, output_list.reshape(-1, features)
    )

    def backward_tick(carried, tick_index):
        arrived = carried[0]
        buffers = carried[1:]
        offset = tick_index - (sections - 1 - position)
        active = (offset >= 0) & (offset < micro_count)
        slot_index = jnp.clip(offset, 0, micro_count - 1)
        grad_out = jnp.where(is_last, pick_slot(grad_top, slot_index), arrived)

        def backward_compute(kept_activations):
            preactivation_gradients, first_row_gradients, gain_accumulated = kept_activations
            grad_float = grad_out.astype(jnp.float32)
            grad_pre = (grad_float * gelu_slope(pick_slot(preactivation_list, slot_index))).astype(
                jnp.bfloat16
            )
            grad_norm = lax.dot_general(
                grad_pre, weight, contract_last, preferred_element_type=jnp.float32
            )
            normed, scale_inv, rounded = normalize(pick_slot(input_list, slot_index), gain_row)
            grad_in, gain_part = norm_back(grad_norm, normed, scale_inv, gain_row)
            sent_output = (grad_float + grad_in).astype(jnp.bfloat16)
            kept_activations = (
                place_slot(preactivation_gradients, grad_pre, slot_index),
                place_slot(first_row_gradients, sent_output, slot_index),
                gain_accumulated + gain_part,
            )
            return (kept_activations, sent_output)

        def backward_bypass(kept_activations):
            return (kept_activations, empty_rows)

        buffers, sent_output = lax.cond(active, backward_compute, backward_bypass, buffers)
        arrived = passed_along(sent_output, "section", -1)
        return ((arrived,) + buffers, None)

    back_state = (empty_rows, zeros_stash, zeros_stash, jnp.zeros((features,), jnp.float32))
    back_final, unused_back = lax.scan(
        backward_tick, back_state, jnp.arange(tick_count, dtype=jnp.int32)
    )
    preactivation_gradients, first_row_gradients, gain_accumulated = back_final[1:]
    pres_flat = preactivation_gradients.reshape(-1, features)
    rounded_flat = rounded_list.reshape(-1, features)
    weight_part = lax.psum_scatter(
        lax.dot_general(
            rounded_flat, pres_flat, contract_first, preferred_element_type=jnp.float32
        ).astype(jnp.bfloat16),
        ("rep", "sub"),
        scatter_dimension=0,
        tiled=True,
    ).astype(jnp.float32)
    gain_total = lax.psum(gain_accumulated, ("rep", "sub"))
    final_total = lax.psum(final_part, ("section", "rep", "sub"))
    embed_in = lax.dot_general(
        onehot_in,
        first_row_gradients.reshape(-1, features),
        contract_first,
        preferred_element_type=jnp.float32,
    )
    contribution = jnp.where(is_first, embed_in, 0.0) + embed_head
    embed_total = lax.psum_scatter(
        contribution, ("section", "rep", "sub"), scatter_dimension=0, tiled=True
    )
    return (weight_part[None], gain_total[None], embed_total, final_total)


def solution(mesh):
    in_specs = (
        P(None, ("rep", "sub")),
        P(None, ("rep", "sub")),
        P(("rep", "sub"), None),
        P("section", ("rep", "sub"), None),
        P("section", None),
        P(),
    )
    out_specs = (
        P("section", ("rep", "sub"), None),
        P("section", None),
        P(("section", "rep", "sub"), None),
        P(),
    )
    return jax.shard_map(body, mesh=mesh, in_specs=in_specs, out_specs=out_specs, check_vma=False)
```

profile of v0, /device:TPU:8, one launch (start us, length us, event | category | flops | bytes accessed | tf_op | source)
XLA Modules:
  0.0 1360.2 jit_solution(7029663618918827461)
XLA Ops:
  9.5 84.1 %all-gather.3.cloned.1.call-done = bf16[256,2048]{1,0:T(8,128)(2,1)} async-done(((bf16[16,2048]{1,0:T(8,128)(2,1)}), bf16[256,2048]{1,0:T(8,128)(2,1)}) %all-gather.3.cloned.1.call-update) | async-done | bytes 1048592 | tf_op jit(solution)/shard_map/all_gather | solution.py:67
  96.3 99.8 %all-gather.5.cloned.1.call-done = bf16[1,2048,2048]{2,1,0:T(8,128)(2,1)} async-done(((bf16[1,128,2048]{2,1,0:T(8,128)(2,1)}), bf16[1,2048,2048]{2,1,0:T(8,128)(2,1)}) %all-gather.5.cloned.1.call-update) | async-done | bytes 8388624 | tf_op jit(solution)/shard_map/all_gather | solution.py:68
  199.0 350.3 %while.36 = (s32[]{:T(128)}, bf16[32,2048]{1,0:T(8,128)(2,1)S(1)}, bf16[8,32,2048]{2,1,0:T(8,128)(2,1)S(1)}, bf16[8,32,2048]{2,1,0:T(8,128)(2,1)}, f32[8,32,2048...) while((s32[]{:T(128)}, bf16[32,2048]{1,0:T(8,128)(2,1)S(1)}, ...), condition=%wide.region_4.5_spmd, body=%wide.region_0.4_spmd.sunk | while | flops 269877280 | bytes 10897188 | solution.py:111
  202.2 10.6 collective-permute-done
  216.0 10.6 collective-permute-done
  229.8 9.2 collective-permute-done
  242.2 11.5 collective-permute-done
  264.3 9.2 collective-permute-done
  284.0 9.2 collective-permute-done
  303.8 9.2 collective-permute-done
  323.6 9.2 collective-permute-done
  343.3 9.2 collective-permute-done
  363.0 9.2 collective-permute-done
  382.8 9.2 collective-permute-done
  402.5 9.8 collective-permute-done
  415.6 9.5 collective-permute-done
  428.4 9.3 collective-permute-done
  440.9 9.2 collective-permute-done
  453.3 9.2 collective-permute-done
  465.7 9.2 collective-permute-done
  478.1 9.2 collective-permute-done
  490.5 9.2 collective-permute-done
  502.9 9.2 collective-permute-done
  515.3 9.2 collective-permute-done
  527.7 9.2 collective-permute-done
  540.1 9.2 collective-permute-done
  553.5 419.2 %while.37 = (s32[]{:T(128)}, bf16[32,2048]{1,0:T(8,128)(2,1)S(1)}, bf16[8,32,2048]{2,1,0:T(8,128)(2,1)}, bf16[8,32,2048]{2,1,0:T(8,128)(2,1)}, f32[2048]{0:T(102...) while((s32[]{:T(128)}, bf16[32,2048]{1,0:T(8,128)(2,1)S(1)}, ...), condition=%wide.region_17.18_spmd, body=%wide.region_11.17_spmd.sunk | while | flops 271122464 | bytes 11323943 | solution.py:183
  680.6 60.2 %collective-permute-done.1 = bf16[32,2048]{1,0:T(8,128)(2,1)S(1)} collective-permute-done((bf16[32,2048]{1,0:T(8,128)(2,1)S(1)}, bf16[32,2048]{1,0:T(8,128)(2,1)S(1)}, u32[]{:S(2)}, u32[]{:S(2)}) %collective-permute-start.1) | collective-permute-done | bytes 131104 | tf_op jit(solution)/shard_map/while/body/eval_jaxpr/ppermute | solution.py:14
  742.0 9.8 conditional.7
  753.7 9.2 collective-permute-done.1
  764.2 9.8 conditional.7
  775.9 9.2 collective-permute-done.1
  786.3 9.8 conditional.7
  798.1 9.2 collective-permute-done.1
  808.5 9.8 conditional.7
  820.2 9.2 collective-permute-done.1
  830.6 9.8 conditional.7
  842.4 9.2 collective-permute-done.1
  852.8 9.8 conditional.7
  864.5 9.2 collective-permute-done.1
  874.9 9.8 conditional.7
  886.6 10.3 collective-permute-done.1
  898.2 9.8 conditional.7
  913.7 18.4 %collective-permute-start.1 = (bf16[32,2048]{1,0:T(8,128)(2,1)S(1)}, bf16[32,2048]{1,0:T(8,128)(2,1)S(1)}, u32[]{:S(2)}, u32[]{:S(2)}) collective-permute-start(bf16[32,2048]{1,0:T(8,128)(2,1)S(1)} %get-tuple-element.740), channel_id=1, source_target_pairs={{16,0},{32,16},{48,32},{64,48},{80,64},{96,80},{112,96},{128,112},... | collective-permute-start | bytes 393224 | tf_op jit(solution)/shard_map/while/body/eval_jaxpr/ppermute | solution.py:14
  983.0 82.7 %psum.15 = f32[2048]{0:T(1024)} all-reduce(f32[2048]{0:T(1024)S(1)} %get-tuple-element.500), channel_id=1, replica_groups=mesh['section'=16,'rep'=4,'sub'=4] {'section','rep','sub'}, use_global_device_ids=true, to_apply=%region_21.22 | all-reduce | flops 2048 | bytes 16384 | tf_op jit(solution)/shard_map/psum | solution.py:198
  1065.7 40.4 %psum.14 = f32[1,2048]{1,0:T(1,128)} all-reduce(f32[1,2048]{1,0:T(1,128)S(1)} %bitcast.89), channel_id=1, replica_groups=mesh['section'=16,'rep'=4,'sub'=4] {'rep','sub'}, use_global_device_ids=true, to_apply=%region_19.20 | all-reduce | flops 2048 | bytes 16384 | tf_op jit(solution)/shard_map/psum | solution.py:197
  1106.1 136.6 %all-reduce.3.cloned.1.call-done = f32[256,2048]{1,0:T(8,128)} async-done(((f32[256,2048]{1,0:T(8,128)}), f32[256,2048]{1,0:T(8,128)}) %all-reduce.3.cloned.1.call-update) | async-done | bytes 2097168
  1244.2 107.4 %reduce-scatter.2.cloned.1.call-done = bf16[128,2048]{1,0:T(8,128)(2,1)} async-done(((bf16[2048,2048]{1,0:T(8,128)(2,1)}), bf16[128,2048]{1,0:T(8,128)(2,1)}) %reduce-scatter.2.cloned.1.call-update) | async-done | bytes 524304 | tf_op jit(solution)/shard_map/reduce_scatter | solution.py:189
  (310 shorter events, 464.0 us)
Async XLA Ops:
  7.2 86.4 %all-gather.3.cloned.1.call-start = ((), (), s32[]{:S(2)}) async-start(), calls=%async_computation.1 | async-start | bytes 1114112 | tf_op jit(solution)/shard_map/all_gather | solution.py:67
  7.9 188.1 %all-gather.5.cloned.1.call-start = ((), (), s32[]{:S(2)}) async-start(), calls=%async_computation.2 | async-start | bytes 8912896 | tf_op jit(solution)/shard_map/all_gather | solution.py:68
  8.6 1234.1 %all-reduce.3.cloned.1.call-start = ((), (), s32[]{:S(2)}) async-start(), calls=%async_computation.4 | async-start | bytes 4194304
  200.3 12.5 collective-permute-start
  214.1 12.5 collective-permute-start
  227.9 11.1 collective-permute-start
  240.3 13.4 collective-permute-start
  262.4 11.1 collective-permute-start
  282.1 11.1 collective-permute-start
  301.9 11.1 collective-permute-start
  321.6 11.1 collective-permute-start
  341.4 11.1 collective-permute-start
  361.1 11.1 collective-permute-start
  380.9 11.1 collective-permute-start
  400.6 11.7 collective-permute-start
  413.7 11.5 collective-permute-start
  426.4 11.2 collective-permute-start
  438.9 11.1 collective-permute-start
  451.4 11.1 collective-permute-start
  463.8 11.1 collective-permute-start
  476.2 11.1 collective-permute-start
  488.6 11.1 collective-permute-start
  501.0 11.1 collective-permute-start
  513.4 11.1 collective-permute-start
  525.8 11.1 collective-permute-start
  538.2 11.1 collective-permute-start
  560.5 11.1 collective-permute-start.1
  572.9 11.1 collective-permute-start.1
  585.3 11.1 collective-permute-start.1
  597.7 11.1 collective-permute-start.1
  610.1 11.1 collective-permute-start.1
  622.4 11.1 collective-permute-start.1
  634.8 11.1 collective-permute-start.1
  647.2 11.1 collective-permute-start.1
  659.6 11.1 collective-permute-start.1
  672.0 68.8 %collective-permute-start.1 = (bf16[32,2048]{1,0:T(8,128)(2,1)S(1)}, bf16[32,2048]{1,0:T(8,128)(2,1)S(1)}, u32[]{:S(2)}, u32[]{:S(2)}) collective-permute-start(bf16[32,2048]{1,0:T(8,128)(2,1)S(1)} %get-tuple-element.740), channel_id=1, source_target_pairs={{16,0},{32,16},{48,32},{64,48},{80,64},{96,80},{112,96},{128,112},... | collective-permute-start | bytes 393224 | tf_op jit(solution)/shard_map/while/body/eval_jaxpr/ppermute | solution.py:14
  751.8 11.1 collective-permute-start.1
  774.0 11.1 collective-permute-start.1
  796.2 11.1 collective-permute-start.1
  818.3 11.1 collective-permute-start.1
  840.4 11.1 collective-permute-start.1
  862.6 11.1 collective-permute-start.1
  884.7 12.3 collective-permute-start.1
  913.7 21.7 %collective-permute-start.1 = (bf16[32,2048]{1,0:T(8,128)(2,1)S(1)}, bf16[32,2048]{1,0:T(8,128)(2,1)S(1)}, u32[]{:S(2)}, u32[]{:S(2)}) collective-permute-start(bf16[32,2048]{1,0:T(8,128)(2,1)S(1)} %get-tuple-element.740), channel_id=1, source_target_pairs={{16,0},{32,16},{48,32},{64,48},{80,64},{96,80},{112,96},{128,112},... | collective-permute-start | bytes 393224 | tf_op jit(solution)/shard_map/while/body/eval_jaxpr/ppermute | solution.py:14
  936.7 11.1 collective-permute-start.1
  949.1 11.1 collective-permute-start.1
  961.5 11.1 collective-permute-start.1
  975.8 375.7 %reduce-scatter.2.cloned.1.call-start = ((), (), s32[]{:S(2)}) async-start(), calls=%async_computation.3 | async-start | bytes 8912896 | tf_op jit(solution)/shard_map/reduce_scatter | solution.py:189
  (11 other events, 1740.2 us)
Sparse Core Ops, SparseCore 0:
  9.8 83.7 all-gather.2
  95.4 100.6 all-gather.4
  975.9 266.7 all-reduce.2
  1245.1 106.3 reduce-scatter.1
where the time goes:
time: 1360 us
  waiting for transfers between devices  810 us (60%)
  starting transfers between devices  191 us (14%)
  blocking collectives  123 us (9%)
  matrix products  105 us (8%)
  local copies, waits for them, and re-layouts  44.2 us (3%)
  other arithmetic  40.1 us (3%)
  loops' own time  32.3 us (2%)
  between operations  13.9 us (1%)
    ppermute x46, waiting for transfers between devices, passed_along(): lax.ppermute(value, axis, [(source, source + steps) for source in range(i...  381 us
    ppermute x46, starting transfers between devices, passed_along(): lax.ppermute(value, axis, [(source, source + steps) for source in range(i...  191 us
    unnamed x5, waiting for transfers between devices  138 us
    reduce_scatter x1, waiting for transfers between devices, body(): lax.psum_scatter(lax.dot_general(rounded_flat, pres_flat, contract_first,...  107 us
    all_gather x1, waiting for transfers between devices, body(): lax.all_gather(section_weight, ('rep', 'sub'), axis=1, tiled=True)[0]  99.8 us
    all_gather x1, waiting for transfers between devices, body(): vocab_table = lax.all_gather(embedding, ('rep', 'sub'), axis=0, tiled=True)  84.1 us
    psum x1, blocking collectives, body(): final_total = lax.psum(final_part, ('section', 'rep', 'sub'))  82.7 us
    dot_general x8, matrix products, backward_compute(): lax.dot_general(grad_pre, weight, contract_last, preferred_element_type=j...  48.8 us
  transfers between devices with their start and end apart: 50, of which 50 were waited for; matrix products, arithmetic and copies ran while one was open for 1% of the time, Pallas kernels for 0%

commit v1 on v0

--- a/solution.py
+++ b/solution.py
@@ -64,7 +64,8 @@
     tick_count = micro_count + sections - 1
     contract_last = (((1,), (1,)), ((), ()))
     contract_first = (((0,), (0,)), ((), ()))
-    vocab_table = lax.all_gather(embedding, ("rep", "sub"), axis=0, tiled=True)
+    stack = jnp.stack([embedding] * lax.axis_size(("rep", "sub")))
+    vocab_table = jnp.concatenate(lax.all_to_all(stack, ("rep", "sub"), 0, 0), axis=0)
     weight = lax.all_gather(section_weight, ("rep", "sub"), axis=1, tiled=True)[0]
     gain_row = section_gain[0]
     is_first = position == 0

time: 1360 us -> 1300 us (0.956)
  waiting for transfers between devices: 810 us -> 734 us
    all_to_all x0 -> x1, waiting for transfers between devices: none -> 109 us  [body(): lax.all_to_all(stack, ('rep', 'sub'), 0, 0)]
    all_gather x1, waiting for transfers between devices: 99.8 us -> 0.01 us  [body(): lax.all_gather(section_weight, ('rep', 'sub'), axis=1, tiled=True)[0]]
    all_gather x1 -> x0, waiting for transfers between devices: 84.1 us -> none  [body(): vocab_table = lax.all_gather(embedding, ('rep', 'sub'), axis=0, tiled=True)]
    unnamed x5 -> x4, waiting for transfers between devices: 138 us -> 136 us
  transfers between devices with their start and end apart: 50 -> 50, of which waited for: 50 -> 49; matrix products, arithmetic and copies ran while one was open for 1% -> 1% of each run, Pallas kernels for 0% -> 0%
where the time goes in v1:
time: 1300 us
  waiting for transfers between devices  734 us (56%)
  starting transfers between devices  200 us (15%)
  blocking collectives  130 us (10%)
  matrix products  103 us (8%)
  local copies, waits for them, and re-layouts  44.9 us (3%)
  other arithmetic  42.6 us (3%)
  loops' own time  30.8 us (2%)
  between operations  13.9 us (1%)
    ppermute x46, waiting for transfers between devices, passed_along(): lax.ppermute(value, axis, [(source, source + steps) for source in range(i...  382 us
    ppermute x46, starting transfers between devices, passed_along(): lax.ppermute(value, axis, [(source, source + steps) for source in range(i...  192 us
    unnamed x4, waiting for transfers between devices  136 us
    all_to_all x1, waiting for transfers between devices, body(): lax.all_to_all(stack, ('rep', 'sub'), 0, 0)  109 us
    reduce_scatter x1, waiting for transfers between devices, body(): lax.psum_scatter(lax.dot_general(rounded_flat, pres_flat, contract_first,...  107 us
    psum x1, blocking collectives, body(): final_total = lax.psum(final_part, ('section', 'rep', 'sub'))  86.4 us
    dot_general x8, matrix products, backward_compute(): lax.dot_general(grad_pre, weight, contract_last, preferred_element_type=j...  48.9 us
    dot_general x8, matrix products, forward_compute(): pre_act = jnp.dot(rounded, weight, preferred_element_type=jnp.float32)  44.8 us
  transfers between devices with their start and end apart: 50, of which 49 were waited for; matrix products, arithmetic and copies ran while one was open for 1% of the time, Pallas kernels for 0%

profile of v1, /device:TPU:8, one launch (start us, length us, event | category | flops | bytes accessed | tf_op | source)
XLA Modules:
  0.0 1299.0 jit_solution(17838747183885664201)
XLA Ops:
  18.5 108.7 %all-to-all-done = bf16[16,16,2048]{2,1,0:T(8,128)(2,1)S(1)} async-done(((bf16[16,16,2048]{2,1,0:T(8,128)(2,1)}), bf16[16,16,2048]{2,1,0:T(8,128)(2,1)S(1)}, u32[]{:S(2)}, u32[]{:S(2)}) %all-to-all-start) | async-done | bytes 1048608 | tf_op jit(solution)/shard_map/all_to_all | solution.py:68
  131.6 348.6 %while.36 = (s32[]{:T(128)}, bf16[32,2048]{1,0:T(8,128)(2,1)S(1)}, bf16[8,32,2048]{2,1,0:T(8,128)(2,1)S(1)}, bf16[8,32,2048]{2,1,0:T(8,128)(2,1)}, f32[8,32,2048...) while((s32[]{:T(128)}, bf16[32,2048]{1,0:T(8,128)(2,1)S(1)}, ...), condition=%wide.region_4.5_spmd, body=%wide.region_0.4_spmd.sunk | while | flops 269877280 | bytes 10897188 | solution.py:112
  134.8 9.2 collective-permute-done
  147.2 9.2 collective-permute-done
  159.5 9.2 collective-permute-done
  171.8 14.2 %collective-permute-done = bf16[32,2048]{1,0:T(8,128)(2,1)S(1)} collective-permute-done((bf16[32,2048]{1,0:T(8,128)(2,1)S(1)}, bf16[32,2048]{1,0:T(8,128)(2,1)S(1)}, u32[]{:S(2)}, u32[]{:S(2)}) %collective-permute-start) | collective-permute-done | bytes 131104 | tf_op jit(solution)/shard_map/while/body/eval_jaxpr/ppermute | solution.py:14
  196.5 9.2 collective-permute-done
  216.2 9.2 collective-permute-done
  235.8 9.2 collective-permute-done
  255.5 9.2 collective-permute-done
  275.1 9.2 collective-permute-done
  294.8 9.2 collective-permute-done
  314.5 10.7 collective-permute-done
  335.6 9.3 collective-permute-done
  348.0 9.2 collective-permute-done
  360.3 9.2 collective-permute-done
  372.6 9.2 collective-permute-done
  384.9 9.2 collective-permute-done
  397.2 9.2 collective-permute-done
  409.5 9.2 collective-permute-done
  421.8 9.2 collective-permute-done
  434.1 9.2 collective-permute-done
  446.5 9.2 collective-permute-done
  458.8 9.2 collective-permute-done
  471.1 9.2 collective-permute-done
  484.4 423.2 %while.37 = (s32[]{:T(128)}, bf16[32,2048]{1,0:T(8,128)(2,1)S(1)}, bf16[8,32,2048]{2,1,0:T(8,128)(2,1)}, bf16[8,32,2048]{2,1,0:T(8,128)(2,1)S(1)}, f32[2048]{0:T...) while((s32[]{:T(128)}, bf16[32,2048]{1,0:T(8,128)(2,1)S(1)}, ...), condition=%wide.region_17.18_spmd, body=%wide.region_11.17_spmd.sunk | while | flops 271122464 | bytes 11324200 | solution.py:184
  541.1 8.6 collective-permute-start.1
  611.6 63.0 %collective-permute-done.1 = bf16[32,2048]{1,0:T(8,128)(2,1)S(1)} collective-permute-done((bf16[32,2048]{1,0:T(8,128)(2,1)S(1)}, bf16[32,2048]{1,0:T(8,128)(2,1)S(1)}, u32[]{:S(2)}, u32[]{:S(2)}) %collective-permute-start.1) | collective-permute-done | bytes 131104 | tf_op jit(solution)/shard_map/while/body/eval_jaxpr/ppermute | solution.py:14
  675.8 10.1 conditional.7
  687.9 9.2 collective-permute-done.1
  698.4 10.2 conditional.7
  710.5 9.1 collective-permute-done.1
  720.8 10.1 conditional.7
  733.0 9.1 collective-permute-done.1
  743.3 10.1 conditional.7
  755.5 9.1 collective-permute-done.1
  765.8 10.2 conditional.7
  778.0 9.2 collective-permute-done.1
  788.4 10.2 conditional.7
  800.5 9.2 collective-permute-done.1
  810.9 10.2 conditional.7
  823.0 9.1 collective-permute-done.1
  833.3 10.1 conditional.7
  849.2 18.7 %collective-permute-start.1 = (bf16[32,2048]{1,0:T(8,128)(2,1)S(1)}, bf16[32,2048]{1,0:T(8,128)(2,1)S(1)}, u32[]{:S(2)}, u32[]{:S(2)}) collective-permute-start(bf16[32,2048]{1,0:T(8,128)(2,1)S(1)} %get-tuple-element.740), channel_id=1, source_target_pairs={{16,0},{32,16},{48,32},{64,48},{80,64},{96,80},{112,96},{128,112},... | collective-permute-start | bytes 393224 | tf_op jit(solution)/shard_map/while/body/eval_jaxpr/ppermute | solution.py:14
  916.7 86.4 %psum.15 = f32[2048]{0:T(1024)} all-reduce(f32[2048]{0:T(1024)S(1)} %get-tuple-element.500), channel_id=1, replica_groups=mesh['section'=16,'rep'=4,'sub'=4] {'section','rep','sub'}, use_global_device_ids=true, to_apply=%region_21.22 | all-reduce | flops 2048 | bytes 16384 | tf_op jit(solution)/shard_map/psum | solution.py:199
  1003.1 43.1 %psum.14 = f32[1,2048]{1,0:T(1,128)} all-reduce(f32[1,2048]{1,0:T(1,128)S(1)} %bitcast.91), channel_id=1, replica_groups=mesh['section'=16,'rep'=4,'sub'=4] {'rep','sub'}, use_global_device_ids=true, to_apply=%region_19.20 | all-reduce | flops 2048 | bytes 16384 | tf_op jit(solution)/shard_map/psum | solution.py:198
  1046.2 135.3 %all-reduce.3.cloned.1.call-done = f32[256,2048]{1,0:T(8,128)} async-done(((f32[256,2048]{1,0:T(8,128)}), f32[256,2048]{1,0:T(8,128)}) %all-reduce.3.cloned.1.call-update) | async-done | bytes 2097168
  1182.9 107.5 %reduce-scatter.2.cloned.1.call-done = bf16[128,2048]{1,0:T(8,128)(2,1)} async-done(((bf16[2048,2048]{1,0:T(8,128)(2,1)}), bf16[128,2048]{1,0:T(8,128)(2,1)}) %reduce-scatter.2.cloned.1.call-update) | async-done | bytes 524304 | tf_op jit(solution)/shard_map/reduce_scatter | solution.py:190
  (310 shorter events, 463.5 us)
Async XLA Ops:
  7.2 121.5 %all-gather.2.cloned.1.call-start = ((), (), s32[]{:S(2)}) async-start(), calls=%async_computation.2 | async-start | bytes 8912896 | tf_op jit(solution)/shard_map/all_gather | solution.py:69
  9.8 117.3 %all-to-all-start = ((bf16[16,16,2048]{2,1,0:T(8,128)(2,1)}), bf16[16,16,2048]{2,1,0:T(8,128)(2,1)S(1)}, u32[]{:S(2)}, u32[]{:S(2)}) async-start(bf16[16,16,2048]{2,1,0:T(8,128)(2,1)} %stack.2), calls=%async_computation | async-start | bytes 2097152 | tf_op jit(solution)/shard_map/all_to_all | solution.py:68
  18.3 1163.1 %all-reduce.3.cloned.1.call-start = ((), (), s32[]{:S(2)}) async-start(), calls=%async_computation.4 | async-start | bytes 4194304
  132.9 11.2 collective-permute-start
  145.2 11.1 collective-permute-start
  157.6 11.1 collective-permute-start
  169.9 16.2 %collective-permute-start = (bf16[32,2048]{1,0:T(8,128)(2,1)S(1)}, bf16[32,2048]{1,0:T(8,128)(2,1)S(1)}, u32[]{:S(2)}, u32[]{:S(2)}) collective-permute-start(bf16[32,2048]{1,0:T(8,128)(2,1)S(1)} %get-tuple-element.722), channel_id=1, source_target_pairs={{0,16},{16,32},{32,48},{48,64},{64,80},{80,96},{96,112},{112,128},... | collective-permute-start | bytes 393224 | tf_op jit(solution)/shard_map/while/body/eval_jaxpr/ppermute | solution.py:14
  194.6 11.1 collective-permute-start
  214.3 11.1 collective-permute-start
  233.9 11.1 collective-permute-start
  253.6 11.1 collective-permute-start
  273.2 11.1 collective-permute-start
  292.9 11.1 collective-permute-start
  312.5 12.6 collective-permute-start
  333.7 11.2 collective-permute-start
  346.1 11.1 collective-permute-start
  358.4 11.1 collective-permute-start
  370.7 11.1 collective-permute-start
  383.0 11.1 collective-permute-start
  395.3 11.1 collective-permute-start
  407.6 11.1 collective-permute-start
  419.9 11.1 collective-permute-start
  432.2 11.1 collective-permute-start
  444.5 11.1 collective-permute-start
  456.8 11.1 collective-permute-start
  469.1 11.1 collective-permute-start
  491.5 11.1 collective-permute-start.1
  503.9 11.1 collective-permute-start.1
  516.3 11.1 collective-permute-start.1
  528.6 11.1 collective-permute-start.1
  541.1 11.1 collective-permute-start.1
  553.5 11.1 collective-permute-start.1
  565.8 11.1 collective-permute-start.1
  578.2 11.1 collective-permute-start.1
  590.6 11.1 collective-permute-start.1
  603.0 71.6 %collective-permute-start.1 = (bf16[32,2048]{1,0:T(8,128)(2,1)S(1)}, bf16[32,2048]{1,0:T(8,128)(2,1)S(1)}, u32[]{:S(2)}, u32[]{:S(2)}) collective-permute-start(bf16[32,2048]{1,0:T(8,128)(2,1)S(1)} %get-tuple-element.740), channel_id=1, source_target_pairs={{16,0},{32,16},{48,32},{64,48},{80,64},{96,80},{112,96},{128,112},... | collective-permute-start | bytes 393224 | tf_op jit(solution)/shard_map/while/body/eval_jaxpr/ppermute | solution.py:14
  686.0 11.2 collective-permute-start.1
  708.5 11.0 collective-permute-start.1
  731.0 11.1 collective-permute-start.1
  753.5 11.1 collective-permute-start.1
  776.0 11.1 collective-permute-start.1
  798.5 11.1 collective-permute-start.1
  821.0 11.1 collective-permute-start.1
  849.2 21.2 %collective-permute-start.1 = (bf16[32,2048]{1,0:T(8,128)(2,1)S(1)}, bf16[32,2048]{1,0:T(8,128)(2,1)S(1)}, u32[]{:S(2)}, u32[]{:S(2)}) collective-permute-start(bf16[32,2048]{1,0:T(8,128)(2,1)S(1)} %get-tuple-element.740), channel_id=1, source_target_pairs={{16,0},{32,16},{48,32},{64,48},{80,64},{96,80},{112,96},{128,112},... | collective-permute-start | bytes 393224 | tf_op jit(solution)/shard_map/while/body/eval_jaxpr/ppermute | solution.py:14
  871.7 11.1 collective-permute-start.1
  884.1 11.1 collective-permute-start.1
  896.5 11.1 collective-permute-start.1
  909.5 380.9 %reduce-scatter.2.cloned.1.call-start = ((), (), s32[]{:S(2)}) async-start(), calls=%async_computation.3 | async-start | bytes 8912896 | tf_op jit(solution)/shard_map/reduce_scatter | solution.py:190
  (11 other events, 1147.3 us)
Sparse Core Ops, SparseCore 0:
  9.8 116.7 all-gather.1
  909.6 271.7 all-reduce.2
  1184.0 106.3 reduce-scatter.1
